TPU v7x, 32 devices: a whole 2x2x4 slice. The times are simulated.
32 devices in a mesh: expert: 8 (over z, core), mp: 4 (over y, x).
Axes of the slice: x: 2, y: 2, z: 4, core: 2. Of those that a mesh axis runs over, the one named last changes fastest.
Arguments:
- tokens: bfloat16 [2, 2560, 2048], P(None, 'expert', 'mp'), may hold values from -6 to 6
- expert_index: int32 [2, 2560], P(None, 'expert'), may hold values from 0 to 7
- slot_index: int32 [2, 2560], P(None, 'expert'), may hold values from 0 to 5, as said below
- kept_mask: int32 [2, 2560], P(None, 'expert'), may hold values from 0 to 1
- gate_prob: float32 [2, 2560], P(None, 'expert'), may hold values from 0.2 to 1
- w_in: bfloat16 [8, 2048, 6144], P('expert', None, 'mp'), may hold values from -0.125 to 0.125
- w_out: bfloat16 [8, 6144, 2048], P('expert', 'mp'), may hold values from -0.078125 to 0.078125
Outputs:
- mixed: bfloat16 [2, 2560, 2048], P(None, 'expert', 'mp')
Inputs may be any that keep to these rules, and one draw needn't show every extreme that they name: `slot_index`: within one aligned block of 320 tokens of a group, no two kept tokens share both expert and slot; in every group some expert has all 6 slots of every block taken. Dropped tokens carry a slot value too, which means nothing.
All inputs are finite; a program needn't handle non-finite values.
Results may differ from a plain program's by a relative error of at most 0.018.
Values may be sent and summed in bfloat16 or wider, within the bound.
A program may use at most 64 MiB of HBM per device.

v0:
```python
import jax
import jax.numpy as jnp
from jax import lax
from jax.sharding import PartitionSpec as P

GROUPS = 2
CAP = 6


def slot_table(expert_index, slot_index, kept_mask, experts):
    code = jnp.where(kept_mask > 0, expert_index * CAP + slot_index, -1)
    places = lax.broadcasted_iota(jnp.int32, (experts * CAP, code.shape[0]), 0)
    return (places == code[None, :]).astype(jnp.bfloat16)


def expert_pass(received, w_first, w_second, gather_rows, scatter_sums, send_back):
    source, slots, narrow = received.shape
    flat = received.reshape(source * slots, narrow)
    hidden_width = w_first.shape[1]

    def add_piece(total, piece, start):
        return jnp.dot(piece, w_first, preferred_element_type=jnp.float32)

    pre = gather_rows(flat, add_piece, jnp.zeros((source * slots, hidden_width), jnp.float32))
    hidden = jnp.maximum(pre, 0.0).astype(jnp.bfloat16)
    whole = jnp.dot(hidden, w_second, preferred_element_type=jnp.float32)
    summed = scatter_sums(whole)
    outgoing = summed.astype(jnp.bfloat16).reshape(source, slots, narrow)
    return send_back(outgoing)


def combine(table, returned, gate):
    flat = returned.reshape(returned.shape[0] * returned.shape[1], returned.shape[2])
    picked = lax.dot_general(
        table, flat, (((0,), (0,)), ((), ())), preferred_element_type=jnp.float32
    )
    return (gate[:, None] * picked).astype(jnp.bfloat16)


def on_device(tokens, expert_index, slot_index, kept_mask, gate_prob, w_in, w_out):
    experts = lax.axis_size("expert")
    w_first = w_in[0]
    w_second = w_out[0]
    narrow = tokens.shape[2]
    tables = []
    outgoing = []
    for group in range(GROUPS):
        table = slot_table(expert_index[group], slot_index[group], kept_mask[group], experts)
        tables.append(table)
        packed = jnp.dot(table, tokens[group], preferred_element_type=jnp.float32).astype(
            jnp.bfloat16
        )
        outgoing.append(packed.reshape(experts, CAP, narrow))
    results = []
    stacked = jnp.concatenate(outgoing, axis=1)
    returned = expert_pass(
        lax.all_to_all(stacked, "expert", split_axis=0, concat_axis=0, tiled=True),
        w_first,
        w_second,
        lambda flat, fold, start_value: fold(
            start_value, lax.all_gather(flat, "mp", axis=1, tiled=True), jnp.int32(0)
        ),
        lambda whole: lax.psum_scatter(
            whole.astype(jnp.bfloat16), "mp", scatter_dimension=1, tiled=True
        ).astype(jnp.float32),
        lambda outbound: lax.all_to_all(
            outbound, "expert", split_axis=0, concat_axis=0, tiled=True
        ),
    )
    for group in range(GROUPS):
        own = returned[:, group * CAP : (group + 1) * CAP, :]
        results.append(combine(tables[group], own, gate_prob[group]))
    return jnp.stack(results)


def solution(mesh):
    placed = (
        P(None, "expert", "mp"),
        P(None, "expert"),
        P(None, "expert"),
        P(None, "expert"),
        P(None, "expert"),
        P("expert", None, "mp"),
        P("expert", "mp", None),
    )
    return jax.shard_map(
        on_device, mesh=mesh, in_specs=placed, out_specs=P(None, "expert", "mp"), check_vma=False
    )
```

profile of v0, /device:TPU:0, one launch (start us, length us, event | category | flops | bytes accessed | tf_op | source)
XLA Modules:
  0.0 84.2 jit_solution(15073820139488619911)
XLA Ops:
  6.5 0.0 reduce-scatter.2.cloned.1.call-start
  6.5 0.8 fusion.28
  7.3 1.1 %convolution_convert_fusion.1 = bf16[48,512]{1,0:T(8,128)(2,1)S(1)} fusion(bf16[2,320,512]{2,1,0:T(8,128)(2,1)} %param.7, s32[320]{0:T(512)S(1)} %get-tuple-element.5), kind=kOutput, calls=%fused_computation.14 | convolution fusion | flops 15768576 | bytes 378112 | tf_op jit(solution)/shard_map/dot_general | solution.py:50
  8.5 1.1 %convolution_convert_fusion = bf16[48,512]{1,0:T(8,128)(2,1)S(1)} fusion(bf16[2,320,512]{2,1,0:T(8,128)(2,1)} %param.7, s32[320]{0:T(512)S(1)} %get-tuple-element.6), kind=kOutput, calls=%fused_computation.13 | convolution fusion | flops 15768576 | bytes 378112 | tf_op jit(solution)/shard_map/dot_general | solution.py:50
  9.7 12.9 %all_to_all.10 = bf16[8,12,512]{2,1,0:T(8,128)(2,1)S(1)} all-to-all(bf16[8,12,512]{2,1,0:T(8,128)(2,1)S(1)} %pad_maximum_fusion.1), channel_id=1, replica_groups=mesh['expert'=8,'mp'=4] {'expert'}, dimensions={0} | all-to-all | bytes 196608 | tf_op jit(solution)/shard_map/all_to_all | solution.py:57
  22.7 9.5 %all_gather.3 = bf16[96,2048]{1,0:T(8,128)(2,1)S(1)} all-gather(bf16[96,512]{1,0:T(8,128)(2,1)S(1)} %reshape.22), channel_id=1, replica_groups=mesh['expert'=8,'mp'=4] {'mp'}, dimensions={1}, use_global_device_ids=true | all-gather | bytes 491520 | tf_op jit(solution)/shard_map/all_gather | solution.py:61
  32.2 0.0 copy-start
  32.2 7.5 %fusion.7 = bf16[96,2048]{1,0:T(8,128)(2,1)} fusion(bf16[1,1536,2048]{2,1,0:T(8,128)(2,1)} %param.13, bf16[96,2048]{1,0:T(8,128)(2,1)S(1)} %all_gather.3, bf16[1,2048,1536]{2,1,0:T(8,128)(2,1)} %param.12), kind=kOutput, calls=%fused_computation.5 | convolution fusion | flops 1208451072 | bytes 13369344 | tf_op jit(solution)/shard_map/dot_general | solution.py:26
  39.7 0.0 reduce-scatter.2.cloned.1.call-update
  39.7 23.1 %reduce-scatter.2.cloned.1.call-done = bf16[96,512]{1,0:T(8,128)(2,1)} async-done(((bf16[96,2048]{1,0:T(8,128)(2,1)}), bf16[96,512]{1,0:T(8,128)(2,1)}) %reduce-scatter.2.cloned.1.call-update) | async-done | bytes 98320 | tf_op jit(solution)/shard_map/reduce_scatter | solution.py:63
  62.8 1.6 %reshape.23 = bf16[8,12,512]{2,1,0:T(8,128)(2,1)} reshape(bf16[96,512]{1,0:T(8,128)(2,1)} %reduce-scatter.2.cloned.1.call-done) | data formatting | bytes 196608 | tf_op jit(solution)/shard_map/reshape | solution.py:28
  64.4 4.6 %all-to-all-start.1 = ((bf16[8,12,512]{2,1,0:T(8,128)(2,1)}), bf16[8,12,512]{2,1,0:T(8,128)(2,1)S(1)}, u32[]{:S(2)}, u32[]{:S(2)}) async-start(bf16[8,12,512]{2,1,0:T(8,128)(2,1)} %reshape.23), calls=%async_computation.2 | async-start | bytes 262144 | tf_op jit(solution)/shard_map/all_to_all | solution.py:66
  69.0 0.0 copy-done
  69.0 6.7 %all-to-all-done.1 = bf16[8,12,512]{2,1,0:T(8,128)(2,1)S(1)} async-done(((bf16[8,12,512]{2,1,0:T(8,128)(2,1)}), bf16[8,12,512]{2,1,0:T(8,128)(2,1)S(1)}, u32[]{:S(2)}, u32[]{:S(2)}) %all-to-all-start.1) | async-done | bytes 98336 | tf_op jit(solution)/shard_map/all_to_all | solution.py:66
  75.9 0.3 fusion.15
  76.2 0.3 fusion.16
  76.5 0.9 %pad_maximum_fusion = bf16[2,320,512]{2,1,0:T(8,128)(2,1)} fusion(bf16[1,320,512]{2,1,0:T(8,128)(2,1)S(1)} %fusion.15, bf16[1,320,512]{2,1,0:T(8,128)(2,1)S(1)} %fusion.16), kind=kLoop, calls=%fused_computation.15 | loop fusion | flops 327680 | bytes 1310720 | tf_op jit(solution)/shard_map/stack | solution.py:73
  (8 shorter events, 0.2 us)
Async XLA Ops:
  6.5 56.3 %reduce-scatter.2.cloned.1.call-start = ((), (), s32[]{:S(2)}) async-start(), calls=%async_computation.3 | async-start | bytes 491520 | tf_op jit(solution)/shard_map/reduce_scatter | solution.py:63
  32.2 36.8 %copy-start = (f32[2,320]{1,0:T(2,128)S(1)}, f32[2,320]{1,0:T(2,128)}, u32[]{:S(2)}) copy-start(f32[2,320]{1,0:T(2,128)} %param.11) | copy-start | bytes 7684
  64.4 11.3 %all-to-all-start.1 = ((bf16[8,12,512]{2,1,0:T(8,128)(2,1)}), bf16[8,12,512]{2,1,0:T(8,128)(2,1)S(1)}, u32[]{:S(2)}, u32[]{:S(2)}) async-start(bf16[8,12,512]{2,1,0:T(8,128)(2,1)} %reshape.23), calls=%async_computation.2 | async-start | bytes 262144 | tf_op jit(solution)/shard_map/all_to_all | solution.py:66
Sparse Core Ops, SparseCore 0:
  39.8 22.9 reduce-scatter.1
where the time goes:
time: 84.6 us; the launch traced here: 84.2 us
  waiting for transfers between devices  29.9 us (35%)
  blocking collectives  22.4 us (26%)
  between operations  13.5 us (16%)
  matrix products  10.4 us (12%)
  starting transfers between devices  4.6 us (5%)
  local copies, waits for them, and re-layouts  1.75 us (2%)
  other arithmetic  1.73 us (2%)
    reduce_scatter x1, waiting for transfers between devices, on_device(): lax.psum_scatter(whole.astype(jnp.bfloat16), 'mp', scatter_dimension=1, t...  23.1 us
    all_to_all x1, blocking collectives, on_device(): lax.all_to_all(stacked, 'expert', split_axis=0, concat_axis=0, tiled=True)  12.9 us
    all_gather x1, blocking collectives, on_device(): lax.all_gather(flat, 'mp', axis=1, tiled=True)  9.52 us
    dot_general x1, matrix products, expert_pass(): whole = jnp.dot(hidden, w_second, preferred_element_type=jnp.float32)  7.49 us
    all_to_all x1, waiting for transfers between devices, on_device(): lax.all_to_all(outbound, 'expert', split_axis=0, concat_axis=0, tiled=True)  6.72 us
    all_to_all x1, starting transfers between devices, on_device(): lax.all_to_all(outbound, 'expert', split_axis=0, concat_axis=0, tiled=True)  4.59 us
    dot_general x2, matrix products, on_device(): jnp.dot(table, tokens[group], preferred_element_type=jnp.float32)  2.28 us
  transfers between devices with their start and end apart: 2, of which 2 were waited for; matrix products, arithmetic and copies ran while one was open for 0% of the time, Pallas kernels for 0%

commit v1 on v0

--- a/solution.py
+++ b/solution.py
@@ -5,6 +5,11 @@
 
 GROUPS = 2
 CAP = 6
+
+
+def stack_and_merge(x, axis, dim):
+    tiles = lax.all_gather(x, axis)
+    return jnp.concatenate(tiles, axis=dim)
 
 
 def slot_table(expert_index, slot_index, kept_mask, experts):
@@ -58,7 +63,7 @@
         w_first,
         w_second,
         lambda flat, fold, start_value: fold(
-            start_value, lax.all_gather(flat, "mp", axis=1, tiled=True), jnp.int32(0)
+            start_value, stack_and_merge(flat, "mp", 1), jnp.int32(0)
         ),
         lambda whole: lax.psum_scatter(
             whole.astype(jnp.bfloat16), "mp", scatter_dimension=1, tiled=True

time: 84.6 us -> 84.6 us (level)
  no operation moved by 1% of the time
where the time goes in v1:
time: 84.6 us; the launch traced here: 84.2 us
  waiting for transfers between devices  29.9 us (35%)
  blocking collectives  22.4 us (26%)
  between operations  13.5 us (16%)
  matrix products  10.4 us (12%)
  starting transfers between devices  4.6 us (5%)
  local copies, waits for them, and re-layouts  1.78 us (2%)
  other arithmetic  1.73 us (2%)
    reduce_scatter x1, waiting for transfers between devices, on_device(): lax.psum_scatter(whole.astype(jnp.bfloat16), 'mp', scatter_dimension=1, t...  23.1 us
    all_to_all x1, blocking collectives, on_device(): lax.all_to_all(stacked, 'expert', split_axis=0, concat_axis=0, tiled=True)  12.9 us
    all_gather x1, blocking collectives, stack_and_merge(): tiles = lax.all_gather(x, axis)  9.52 us
    dot_general x1, matrix products, expert_pass(): whole = jnp.dot(hidden, w_second, preferred_element_type=jnp.float32)  7.49 us
    all_to_all x1, waiting for transfers between devices, on_device(): lax.all_to_all(outbound, 'expert', split_axis=0, concat_axis=0, tiled=True)  6.72 us
    all_to_all x1, starting transfers between devices, on_device(): lax.all_to_all(outbound, 'expert', split_axis=0, concat_axis=0, tiled=True)  4.59 us
    dot_general x2, matrix products, on_device(): jnp.dot(table, tokens[group], preferred_element_type=jnp.float32)  2.28 us
  transfers between devices with their start and end apart: 2, of which 2 were waited for; matrix products, arithmetic and copies ran while one was open for 0% of the time, Pallas kernels for 0%

profile of v1, /device:TPU:0, one launch (start us, length us, event | category | flops | bytes accessed | tf_op | source)
XLA Modules:
  0.0 84.2 jit_solution(8524384125262805436)
XLA Ops:
  6.5 0.0 reduce-scatter.2.cloned.1.call-start
  6.5 0.8 fusion.28
  7.3 1.1 %convolution_convert_fusion.1 = bf16[48,512]{1,0:T(8,128)(2,1)S(1)} fusion(bf16[2,320,512]{2,1,0:T(8,128)(2,1)} %param.7, s32[320]{0:T(512)S(1)} %get-tuple-element.5), kind=kOutput, calls=%fused_computation.14 | convolution fusion | flops 15768576 | bytes 378112 | tf_op jit(solution)/shard_map/dot_general | solution.py:55
  8.5 1.1 %convolution_convert_fusion = bf16[48,512]{1,0:T(8,128)(2,1)S(1)} fusion(bf16[2,320,512]{2,1,0:T(8,128)(2,1)} %param.7, s32[320]{0:T(512)S(1)} %get-tuple-element.6), kind=kOutput, calls=%fused_computation.13 | convolution fusion | flops 15768576 | bytes 378112 | tf_op jit(solution)/shard_map/dot_general | solution.py:55
  9.7 12.9 %all_to_all.10 = bf16[8,12,512]{2,1,0:T(8,128)(2,1)S(1)} all-to-all(bf16[8,12,512]{2,1,0:T(8,128)(2,1)S(1)} %pad_maximum_fusion.1), channel_id=1, replica_groups=mesh['expert'=8,'mp'=4] {'expert'}, dimensions={0} | all-to-all | bytes 196608 | tf_op jit(solution)/shard_map/all_to_all | solution.py:62
  22.7 9.5 %all_gather.3 = bf16[4,96,512]{2,1,0:T(8,128)(2,1)S(1)} all-gather(bf16[1,96,512]{2,1,0:T(8,128)(2,1)S(1)} %all_gather_reshape.3), channel_id=1, replica_groups=mesh['expert'=8,'mp'=4] {'mp'}, dimensions={0}, use_global_device_ids=true | all-gather | bytes 491520 | tf_op jit(solution)/shard_map/all_gather | solution.py:11
  32.2 0.0 copy-start
  32.2 7.5 %fusion.7 = bf16[96,2048]{1,0:T(8,128)(2,1)} fusion(bf16[1,1536,2048]{2,1,0:T(8,128)(2,1)} %param.13, bf16[96,2048]{1,0:T(8,128)(2,1)S(1)} %bitcast.30, bf16[1,2048,1536]{2,1,0:T(8,128)(2,1)} %param.12), kind=kOutput, calls=%fused_computation.5 | convolution fusion | flops 1208451072 | bytes 13369344 | tf_op jit(solution)/shard_map/dot_general | solution.py:31
  39.7 0.0 reduce-scatter.2.cloned.1.call-update
  39.8 23.1 %reduce-scatter.2.cloned.1.call-done = bf16[96,512]{1,0:T(8,128)(2,1)} async-done(((bf16[96,2048]{1,0:T(8,128)(2,1)}), bf16[96,512]{1,0:T(8,128)(2,1)}) %reduce-scatter.2.cloned.1.call-update) | async-done | bytes 98320 | tf_op jit(solution)/shard_map/reduce_scatter | solution.py:68
  62.9 1.6 %reshape.27 = bf16[8,12,512]{2,1,0:T(8,128)(2,1)} reshape(bf16[96,512]{1,0:T(8,128)(2,1)} %reduce-scatter.2.cloned.1.call-done) | data formatting | bytes 196608 | tf_op jit(solution)/shard_map/reshape | solution.py:33
  64.5 4.6 %all-to-all-start.1 = ((bf16[8,12,512]{2,1,0:T(8,128)(2,1)}), bf16[8,12,512]{2,1,0:T(8,128)(2,1)S(1)}, u32[]{:S(2)}, u32[]{:S(2)}) async-start(bf16[8,12,512]{2,1,0:T(8,128)(2,1)} %reshape.27), calls=%async_computation.2 | async-start | bytes 262144 | tf_op jit(solution)/shard_map/all_to_all | solution.py:71
  69.1 0.0 copy-done
  69.1 6.7 %all-to-all-done.1 = bf16[8,12,512]{2,1,0:T(8,128)(2,1)S(1)} async-done(((bf16[8,12,512]{2,1,0:T(8,128)(2,1)}), bf16[8,12,512]{2,1,0:T(8,128)(2,1)S(1)}, u32[]{:S(2)}, u32[]{:S(2)}) %all-to-all-start.1) | async-done | bytes 98336 | tf_op jit(solution)/shard_map/all_to_all | solution.py:71
  75.9 0.3 fusion.15
  76.2 0.3 fusion.16
  76.5 0.9 %pad_maximum_fusion = bf16[2,320,512]{2,1,0:T(8,128)(2,1)} fusion(bf16[1,320,512]{2,1,0:T(8,128)(2,1)S(1)} %fusion.15, bf16[1,320,512]{2,1,0:T(8,128)(2,1)S(1)} %fusion.16), kind=kLoop, calls=%fused_computation.15 | loop fusion | flops 327680 | bytes 1310720 | tf_op jit(solution)/shard_map/stack | solution.py:78
  (9 shorter events, 0.3 us)
Async XLA Ops:
  6.5 56.4 %reduce-scatter.2.cloned.1.call-start = ((), (), s32[]{:S(2)}) async-start(), calls=%async_computation.3 | async-start | bytes 491520 | tf_op jit(solution)/shard_map/reduce_scatter | solution.py:68
  32.2 36.8 %copy-start = (f32[2,320]{1,0:T(2,128)S(1)}, f32[2,320]{1,0:T(2,128)}, u32[]{:S(2)}) copy-start(f32[2,320]{1,0:T(2,128)} %param.11) | copy-start | bytes 7684
  64.5 11.3 %all-to-all-start.1 = ((bf16[8,12,512]{2,1,0:T(8,128)(2,1)}), bf16[8,12,512]{2,1,0:T(8,128)(2,1)S(1)}, u32[]{:S(2)}, u32[]{:S(2)}) async-start(bf16[8,12,512]{2,1,0:T(8,128)(2,1)} %reshape.27), calls=%async_computation.2 | async-start | bytes 262144 | tf_op jit(solution)/shard_map/all_to_all | solution.py:71
Sparse Core Ops, SparseCore 0:
  39.9 22.9 reduce-scatter.1
